TPU v7x, 32 devices: a whole 2x2x4 slice. The times are simulated.
32 devices in a mesh: seq: 16 (over z, y, core), dp: 2 (over x).
Axes of the slice: x: 2, y: 2, z: 4, core: 2. Of those that a mesh axis runs over, the one named last changes fastest.
Arguments:
- q_student: bfloat16 [2, 8192, 1536], P('dp', 'seq'), may hold values from -8 to 8
- kv_student: bfloat16 [2, 128, 3072], P('dp', 'seq'), may hold values from -8 to 8
- q_target: bfloat16 [2, 8192, 1536], P('dp', 'seq'), may hold values from -8 to 8
- kv_target: bfloat16 [2, 128, 3072], P('dp', 'seq'), may hold values from -8 to 8
Outputs:
- student_out: bfloat16 [2, 8192, 1536], P('dp', 'seq')
- target_out: bfloat16 [2, 8192, 1536], P('dp', 'seq')
- distill_loss: float32 [], replicated
All inputs are finite; a program needn't handle non-finite values.
Results may differ from a plain program's by a relative error of at most 0.004.
Values may be sent and summed in bfloat16 or wider, within the bound.
A program may use at most 128 MiB of HBM per device.

v0:
```python
import jax
import jax.numpy as jnp
from jax import lax
from jax.sharding import PartitionSpec as P

HEADS = 12
HD = 128


def absorb(query3, carried, incoming):
    running_max, running_sum, running_out = carried
    block_pairs = incoming[0]
    key_rows = block_pairs.shape[0]
    feature_width = HEADS * HD
    key_block = block_pairs[:, :feature_width].reshape(key_rows, HEADS, HD)
    value_block = block_pairs[:, feature_width:].reshape(key_rows, HEADS, HD)
    scores = jnp.einsum("qhd,khd->hqk", query3, key_block, preferred_element_type=jnp.float32) * (
        1.0 / HD**0.5
    )
    new_max = jnp.maximum(running_max, jnp.max(scores, axis=-1))
    shrink = jnp.exp(running_max - new_max)
    exponent = jnp.exp(scores - new_max[:, :, None])
    running_sum = jnp.sum(exponent, axis=-1)
    running_out = jnp.einsum(
        "hqk,khd->hqd",
        exponent.astype(jnp.bfloat16),
        value_block,
        preferred_element_type=jnp.float32,
    )
    return (new_max, running_sum, running_out)


def normalize(carried, query_rows):
    running_max, running_sum, running_out = carried
    mixed_rows = running_out / running_sum[:, :, None]
    return jnp.transpose(mixed_rows, (1, 0, 2)).reshape(query_rows, HEADS * HD)


def body(q_student, kv_student, q_target, kv_target):
    query_rows = q_student.shape[1]
    student_query = q_student[0].reshape(query_rows, HEADS, HD)
    target_query = q_target[0].reshape(query_rows, HEADS, HD)
    initial = (
        jnp.full((HEADS, query_rows), -1e30, jnp.float32),
        jnp.zeros((HEADS, query_rows), jnp.float32),
        jnp.zeros((HEADS, query_rows, HD), jnp.float32),
    )
    student_all = lax.all_gather(kv_student, "seq", axis=1, tiled=True)
    target_all = lax.all_gather(kv_target, "seq", axis=1, tiled=True)
    student_carry = absorb(student_query, initial, student_all)
    target_carry = absorb(target_query, initial, target_all)
    student_rows = normalize(student_carry, query_rows)
    target_rows = normalize(target_carry, query_rows)
    seq_count = lax.axis_size("seq")
    all_tokens = query_rows * seq_count
    position = (lax.axis_index("seq") * query_rows + jnp.arange(query_rows)).astype(jnp.float32)
    weight = 1.0 + 2.0 * position / float(max(all_tokens - 1, 1))
    gap_rows = student_rows - target_rows
    local_term = jnp.sum(weight[:, None] * gap_rows * gap_rows) / float(all_tokens * HEADS * HD)
    clip_term = lax.psum(local_term, "seq")
    distill_loss = lax.psum(clip_term, "dp")
    return (
        student_rows[None].astype(jnp.bfloat16),
        target_rows[None].astype(jnp.bfloat16),
        distill_loss,
    )


def solution(mesh):
    return jax.shard_map(
        body,
        mesh=mesh,
        in_specs=(
            P("dp", "seq", None),
            P("dp", "seq", None),
            P("dp", "seq", None),
            P("dp", "seq", None),
        ),
        out_specs=(P("dp", "seq", None), P("dp", "seq", None), P()),
        check_vma=False,
    )
```

profile of v0, /device:TPU:0, one launch (start us, length us, event | category | flops | bytes accessed | tf_op | source)
XLA Modules:
  0.0 106.9 jit_solution(2824079883674600560)
XLA Ops:
  0.6 25.9 %all_gather.7 = bf16[1,128,3072]{2,1,0:T(8,128)(2,1)S(1)} all-gather(bf16[1,8,3072]{2,1,0:T(8,128)(2,1)} %param.7), channel_id=1, replica_groups=mesh['seq'=16,'dp'=2] {'seq'}, dimensions={1}, use_global_device_ids=true | all-gather | bytes 835584 | tf_op jit(solution)/shard_map/all_gather | solution.py:49
  26.5 0.4 copy.33
  26.9 0.8 fusion.13
  27.7 0.7 copy.32
  28.4 0.0 copy-start.4
  28.4 0.6 multiply_reduce_fusion
  29.1 0.6 fusion.3
  29.6 0.0 copy-done.4
  29.6 0.0 copy-start.6
  29.6 2.5 %bitcast_divide_fusion = f32[512,12,128]{0,2,1:T(8,128)} fusion(bf16[128,12,128]{0,2,1:T(8,128)(2,1)S(1)} %bitcast.31, f32[12,512,128]{1,2,0:T(8,128)S(1)} %get-tuple-element.22, f32[512,12]{0,1:T(8,128)S(1)} %bitcast.33, f32[12,512]{1,0:T(8,128)S(1)} %broadcast_maximum_fusion), kind=kOutput, calls=%fused_computation.2 | convolution fusion | flops 204472320 | bytes 6733824 | tf_op jit(solution)/shard_map/hqk,khd->hqd/dot_general | solution.py:24
  32.2 0.0 copy-done.6
  32.2 19.7 %all_gather.6 = bf16[1,128,3072]{2,1,0:T(8,128)(2,1)S(1)} all-gather(bf16[1,8,3072]{2,1,0:T(8,128)(2,1)S(1)} %copy-done.6), channel_id=1, replica_groups=mesh['seq'=16,'dp'=2] {'seq'}, dimensions={1}, use_global_device_ids=true | all-gather | bytes 835584 | tf_op jit(solution)/shard_map/all_gather | solution.py:48
  51.9 0.4 copy.28
  52.3 0.8 fusion.14
  53.1 1.6 %copy.27 = bf16[1,512,1536]{1,2,0:T(8,128)(2,1)} copy(bf16[1,512,1536]{2,1,0:T(8,128)(2,1)S(1)} %copy-done.1) | data formatting | bytes 3145728 | tf_op args[0]
  54.7 2.0 %multiply_reduce_fusion.1 = (f32[12,512]{1,0:T(8,128)S(1)}, f32[12,512,128]{1,2,0:T(8,128)S(1)}) fusion(bf16[512,12,128]{0,2,1:T(8,128)(2,1)} %bitcast.23, bf16[128,12,128]{0,2,1:T(8,128)(2,1)S(1)} %bitcast.29), kind=kOutput, calls=%fused_computation.7 | convolution fusion | flops 202893312 | bytes 5136384 | tf_op jit(solution)/shard_map/qhd,khd->hqk/dot_general | solution.py:17
  56.7 0.0 copy-start.3
  56.7 0.6 copy-done.5
  57.3 1.2 %fusion.1 = f32[12,512]{1,0:T(8,128)} fusion(f32[12,512,128]{1,2,0:T(8,128)S(1)} %get-tuple-element.20, f32[12,512]{1,0:T(8,128)S(1)} %broadcast_maximum_fusion.1), kind=kLoop, calls=%fused_computation.8 | loop fusion | flops 2353152 | bytes 3194880 | tf_op jit(solution)/shard_map/reduce_sum | solution.py:23
  58.5 6.3 %fusion = (f32[]{:T(128)}, bf16[512,12,128]{0,2,1:T(8,128)(2,1)}, bf16[512,12,128]{0,2,1:T(8,128)(2,1)}) fusion(f32[512,12,128]{0,2,1:T(8,128)} %bitcast_divide_fusion, f32[512]{0:T(512)S(1)} %multiply_add_fusion, f32[512,12]{0,1:T(8,128)} %bitcast.32, bf16[128,12,128]{0,2,1:T(8,128)(2,1)S(1)} %bitcast.30, f32[12,512,128]{1,2,0:T(8,128)S(1)} %get-tuple-element.20, ...), kind=kOutput, calls=%fused_computation.1 | convolution fusion | flops 209190912 | bytes 9881604 | tf_op jit(solution)/shard_map/hqk,khd->hqd/dot_general | solution.py:24
  64.8 2.7 %copy.37 = bf16[1,512,1536]{2,1,0:T(8,128)(2,1)} copy(bf16[1,512,1536]{1,2,0:T(8,128)(2,1)} %bitcast.27) | data formatting | bytes 3145728
  67.5 1.6 %copy.38 = bf16[1,512,1536]{2,1,0:T(8,128)(2,1)} copy(bf16[1,512,1536]{1,2,0:T(8,128)(2,1)S(1)} %bitcast.26) | data formatting | bytes 3145728
  69.7 31.7 %psum.14 = f32[]{:T(128)} all-reduce(f32[]{:T(128)S(6)} %div.39), channel_id=1, replica_groups=mesh['seq'=16,'dp'=2] {'seq'}, use_global_device_ids=true, to_apply=%region_5.0 | all-reduce | flops 1 | bytes 8 | tf_op jit(solution)/shard_map/psum | solution.py:60
  101.4 5.5 %psum.15 = f32[]{:T(128)} all-reduce(f32[]{:T(128)} %psum.14), channel_id=1, replica_groups=mesh['seq'=16,'dp'=2] {'dp'}, use_global_device_ids=true, to_apply=%region_6.0 | all-reduce | flops 1 | bytes 8 | tf_op jit(solution)/shard_map/psum | solution.py:61
  (11 shorter events, 0.0 us)
Async XLA Ops:
  0.6 27.1 %copy-start = (bf16[1,512,1536]{2,1,0:T(8,128)(2,1)S(1)}, bf16[1,512,1536]{2,1,0:T(8,128)(2,1)}, u32[]{:S(2)}) copy-start(bf16[1,512,1536]{2,1,0:T(8,128)(2,1)} %param.6) | copy-start | bytes 4718596
  28.4 1.2 %copy-start.4 = (bf16[128,1536]{0,1:T(8,128)(2,1)S(1)}, bf16[128,1536]{0,1:T(8,128)(2,1)}, u32[]{:S(2)}) copy-start(bf16[128,1536]{0,1:T(8,128)(2,1)} %get-tuple-element.16) | copy-start | bytes 1179652
  29.6 2.5 %copy-start.6 = (bf16[1,8,3072]{2,1,0:T(8,128)(2,1)S(1)}, bf16[1,8,3072]{2,1,0:T(8,128)(2,1)}, u32[]{:S(2)}) copy-start(bf16[1,8,3072]{2,1,0:T(8,128)(2,1)} %param.5) | copy-start | bytes 147460
  32.2 20.9 %copy-start.1 = (bf16[1,512,1536]{2,1,0:T(8,128)(2,1)S(1)}, bf16[1,512,1536]{2,1,0:T(8,128)(2,1)}, u32[]{:S(2)}) copy-start(bf16[1,512,1536]{2,1,0:T(8,128)(2,1)} %param.4) | copy-start | bytes 4718596
  56.7 1.8 %copy-start.3 = (bf16[128,1536]{0,1:T(8,128)(2,1)S(1)}, bf16[128,1536]{0,1:T(8,128)(2,1)}, u32[]{:S(2)}) copy-start(bf16[128,1536]{0,1:T(8,128)(2,1)} %get-tuple-element.18) | copy-start | bytes 1179652
  56.7 0.6 copy-start.5
  64.8 2.7 %copy-start.2 = (bf16[512,12,128]{0,2,1:T(8,128)(2,1)S(1)}, bf16[512,12,128]{0,2,1:T(8,128)(2,1)}, u32[]{:S(2)}) copy-start(bf16[512,12,128]{0,2,1:T(8,128)(2,1)} %get-tuple-element.13) | copy-start | bytes 4718596
where the time goes:
time: 107 us
  blocking collectives  82.8 us (77%)
  matrix products  11.5 us (11%)
  local copies, waits for them, and re-layouts  9.49 us (9%)
  other arithmetic  1.75 us (2%)
  between operations  1.39 us (1%)
    psum x1, blocking collectives, body(): clip_term = lax.psum(local_term, 'seq')  31.7 us
    all_gather x1, blocking collectives, body(): target_all = lax.all_gather(kv_target, 'seq', axis=1, tiled=True)  25.9 us
    all_gather x1, blocking collectives, body(): student_all = lax.all_gather(kv_student, 'seq', axis=1, tiled=True)  19.7 us
    dot_general x2, matrix products, absorb(): jnp.einsum('hqk,khd->hqd', exponent.astype(jnp.bfloat16), value_block, pr...  8.79 us
    unnamed x18, local copies, waits for them, and re-layouts  7.15 us
    psum x1, blocking collectives, body(): distill_loss = lax.psum(clip_term, 'dp')  5.54 us
    dot_general x2, matrix products, absorb(): jnp.einsum('qhd,khd->hqk', query3, key_block, preferred_element_type=jnp....  2.66 us

commit v1 on v0

--- a/solution.py
+++ b/solution.py
@@ -45,7 +45,7 @@
         jnp.zeros((HEADS, query_rows), jnp.float32),
         jnp.zeros((HEADS, query_rows, HD), jnp.float32),
     )
-    student_all = lax.all_gather(kv_student, "seq", axis=1, tiled=True)
+    student_all = jnp.concatenate(lax.all_gather(kv_student, "seq"), axis=1)
     target_all = lax.all_gather(kv_target, "seq", axis=1, tiled=True)
     student_carry = absorb(student_query, initial, student_all)
     target_carry = absorb(target_query, initial, target_all)

time: 107 us -> 109 us (1.019)
  other arithmetic: 1.75 us -> 3.1 us
    unnamed x18 -> x16, local copies, waits for them, and re-layouts: 7.15 us -> 6.57 us
where the time goes in v1:
time: 109 us
  blocking collectives  82.8 us (76%)
  matrix products  11.6 us (11%)
  local copies, waits for them, and re-layouts  9.67 us (9%)
  other arithmetic  3.1 us (3%)
  between operations  1.39 us (1%)
    psum x1, blocking collectives, body(): clip_term = lax.psum(local_term, 'seq')  31.7 us
    all_gather x1, blocking collectives, body(): target_all = lax.all_gather(kv_target, 'seq', axis=1, tiled=True)  25.9 us
    all_gather x1, blocking collectives, body(): student_all = jnp.concatenate(lax.all_gather(kv_student, 'seq'), axis=1)  19.7 us
    dot_general x2, matrix products, absorb(): jnp.einsum('hqk,khd->hqd', exponent.astype(jnp.bfloat16), value_block, pr...  8.94 us
    unnamed x16, local copies, waits for them, and re-layouts  6.57 us
    psum x1, blocking collectives, body(): distill_loss = lax.psum(clip_term, 'dp')  5.54 us
    dot_general x2, matrix products, absorb(): jnp.einsum('qhd,khd->hqk', query3, key_block, preferred_element_type=jnp....  2.67 us
    reduce_sum x2, other arithmetic, absorb(): running_sum = jnp.sum(exponent, axis=-1)  2.49 us

profile of v1, /device:TPU:0, one launch (start us, length us, event | category | flops | bytes accessed | tf_op | source)
XLA Modules:
  0.0 108.6 jit_solution(135253588734704774)
XLA Ops:
  0.6 25.9 %all_gather.11 = bf16[1,128,3072]{2,1,0:T(8,128)(2,1)S(1)} all-gather(bf16[1,8,3072]{2,1,0:T(8,128)(2,1)} %param.7), channel_id=1, replica_groups=mesh['seq'=16,'dp'=2] {'seq'}, dimensions={1}, use_global_device_ids=true | all-gather | bytes 835584 | tf_op jit(solution)/shard_map/all_gather | solution.py:49
  26.5 0.4 copy.47
  26.9 0.8 fusion.13
  27.7 0.7 copy.46
  28.4 0.0 copy-start.4
  28.4 0.6 multiply_reduce_fusion
  29.1 0.6 fusion.3
  29.6 0.0 copy-done.4
  29.6 0.0 copy-start.5
  29.6 2.6 %bitcast_divide_fusion = f32[512,12,128]{0,2,1:T(8,128)} fusion(bf16[128,12,128]{0,2,1:T(8,128)(2,1)S(1)} %bitcast.31, f32[12,512,128]{1,2,0:T(8,128)S(1)} %get-tuple-element.25, f32[512,12]{0,1:T(8,128)S(1)} %bitcast.33, f32[12,512]{1,0:T(8,128)S(1)} %broadcast_maximum_fusion), kind=kOutput, calls=%fused_computation.2 | convolution fusion | flops 204472320 | bytes 6733824 | tf_op jit(solution)/shard_map/hqk,khd->hqd/dot_general | solution.py:24
  32.2 19.7 %all-gather = bf16[16,8,3072]{2,1,0:T(8,128)(2,1)S(1)} all-gather(bf16[1,8,3072]{2,1,0:T(8,128)(2,1)S(1)} %copy-done.5), channel_id=2, replica_groups=mesh['seq'=16,'dp'=2] {'seq'}, dimensions={0}, use_global_device_ids=true | all-gather | bytes 835584 | tf_op jit(solution)/shard_map/all_gather | solution.py:48
  51.9 0.8 fusion.14
  52.7 0.2 copy.41
  53.0 1.6 %copy.40 = bf16[1,512,1536]{1,2,0:T(8,128)(2,1)} copy(bf16[1,512,1536]{2,1,0:T(8,128)(2,1)S(1)} %copy-done.1) | data formatting | bytes 3145728 | tf_op args[0]
  54.5 2.0 %multiply_reduce_fusion.1 = (f32[12,512]{1,0:T(8,128)S(1)}, f32[12,512,128]{1,2,0:T(8,128)S(1)}) fusion(bf16[512,12,128]{0,2,1:T(8,128)(2,1)} %bitcast.23, bf16[128,12,128]{0,2,1:T(8,128)(2,1)S(1)} %bitcast.29), kind=kOutput, calls=%fused_computation.7 | convolution fusion | flops 202893312 | bytes 5136384 | tf_op jit(solution)/shard_map/qhd,khd->hqk/dot_general | solution.py:17
  56.6 0.0 copy-start.3
  56.6 0.6 broadcast_maximum_fusion.1
  57.2 1.9 %fusion.1 = f32[12,512]{1,0:T(8,128)} fusion(f32[12,512,128]{1,2,0:T(8,128)S(1)} %get-tuple-element.23, f32[12,512]{1,0:T(8,128)} %broadcast_maximum_fusion.1), kind=kLoop, calls=%fused_computation.8 | loop fusion | flops 2353152 | bytes 3194880 | tf_op jit(solution)/shard_map/reduce_sum | solution.py:23
  59.1 0.9 copy.44
  60.0 6.4 %fusion = (f32[]{:T(128)}, bf16[512,12,128]{0,2,1:T(8,128)(2,1)}, bf16[512,12,128]{0,2,1:T(8,128)(2,1)}) fusion(f32[512,12,128]{0,2,1:T(8,128)} %bitcast_divide_fusion, f32[512]{0:T(512)S(1)} %multiply_add_fusion, f32[512,12]{0,1:T(8,128)} %bitcast.32, bf16[128,12,128]{0,2,1:T(8,128)(2,1)} %bitcast.30, f32[12,512,128]{1,2,0:T(8,128)S(1)} %get-tuple-element.23, ...), kind=kOutput, calls=%fused_computation.1 | convolution fusion | flops 209190912 | bytes 9881604 | tf_op jit(solution)/shard_map/hqk,khd->hqd/dot_general | solution.py:24
  66.4 2.7 %copy.51 = bf16[1,512,1536]{2,1,0:T(8,128)(2,1)} copy(bf16[1,512,1536]{1,2,0:T(8,128)(2,1)} %bitcast.27) | data formatting | bytes 3145728
  69.1 1.6 %copy.52 = bf16[1,512,1536]{2,1,0:T(8,128)(2,1)} copy(bf16[1,512,1536]{1,2,0:T(8,128)(2,1)S(1)} %bitcast.26) | data formatting | bytes 3145728
  71.3 31.7 %psum.14 = f32[]{:T(128)} all-reduce(f32[]{:T(128)S(6)} %div.39), channel_id=1, replica_groups=mesh['seq'=16,'dp'=2] {'seq'}, use_global_device_ids=true, to_apply=%region_5.0 | all-reduce | flops 1 | bytes 8 | tf_op jit(solution)/shard_map/psum | solution.py:60
  103.1 5.5 %psum.15 = f32[]{:T(128)} all-reduce(f32[]{:T(128)} %psum.14), channel_id=1, replica_groups=mesh['seq'=16,'dp'=2] {'dp'}, use_global_device_ids=true, to_apply=%region_6.0 | all-reduce | flops 1 | bytes 8 | tf_op jit(solution)/shard_map/psum | solution.py:61
  (10 shorter events, 0.0 us)
Async XLA Ops:
  0.6 27.1 %copy-start = (bf16[1,512,1536]{2,1,0:T(8,128)(2,1)S(1)}, bf16[1,512,1536]{2,1,0:T(8,128)(2,1)}, u32[]{:S(2)}) copy-start(bf16[1,512,1536]{2,1,0:T(8,128)(2,1)} %param.6) | copy-start | bytes 4718596
  28.4 1.2 %copy-start.4 = (bf16[128,1536]{0,1:T(8,128)(2,1)S(1)}, bf16[128,1536]{0,1:T(8,128)(2,1)}, u32[]{:S(2)}) copy-start(bf16[128,1536]{0,1:T(8,128)(2,1)} %get-tuple-element.19) | copy-start | bytes 1179652
  29.6 2.6 %copy-start.5 = (bf16[1,8,3072]{2,1,0:T(8,128)(2,1)S(1)}, bf16[1,8,3072]{2,1,0:T(8,128)(2,1)}, u32[]{:S(2)}) copy-start(bf16[1,8,3072]{2,1,0:T(8,128)(2,1)} %param.5) | copy-start | bytes 147460
  32.2 20.7 %copy-start.1 = (bf16[1,512,1536]{2,1,0:T(8,128)(2,1)S(1)}, bf16[1,512,1536]{2,1,0:T(8,128)(2,1)}, u32[]{:S(2)}) copy-start(bf16[1,512,1536]{2,1,0:T(8,128)(2,1)} %param.4) | copy-start | bytes 4718596
  56.6 2.5 %copy-start.3 = (bf16[128,1536]{1,0:T(8,128)(2,1)S(1)}, bf16[128,1536]{1,0:T(8,128)(2,1)}, u32[]{:S(2)}) copy-start(bf16[128,1536]{1,0:T(8,128)(2,1)} %get-tuple-element.21) | copy-start | bytes 1179652
  66.4 2.7 %copy-start.2 = (bf16[512,12,128]{0,2,1:T(8,128)(2,1)S(1)}, bf16[512,12,128]{0,2,1:T(8,128)(2,1)}, u32[]{:S(2)}) copy-start(bf16[512,12,128]{0,2,1:T(8,128)(2,1)} %get-tuple-element.16) | copy-start | bytes 4718596
